TPU v7x, 32 devices: a whole 2x2x4 slice. The times are simulated.
32 devices in a mesh: real: 2 (over y), col: 8 (over z, x), row: 2 (over core).
Axes of the slice: x: 2, y: 2, z: 4, core: 2. Of those that a mesh axis runs over, the one named last changes fastest.
Arguments:
- theta: bfloat16 [512, 16384], P(('real', 'row'), 'col'), parts along dimension 0, may hold values from -6 to 6
- signs: int32 [32768], P(('real', 'col')), parts along dimension 0, may hold values from -1 to 1, as said below
- kept: int32 [1024], replicated, may hold values from 0 to 16383, as said below
Outputs:
- gram: float32 [4, 8, 16, 256], P(('real', 'row'), 'col'), parts along dimension 0
There are 2 independent parts, one for each index of `real`. A program takes and returns all parts, laid end to end along the dimension named above; an argument that names none is the same for every part. Nothing has to cross between parts.
Inputs may be any that keep to these rules, and one draw needn't show every extreme that they name: `signs`: each entry is -1 or 1. `kept`: 1024 distinct column indices.
All inputs are finite; a program needn't handle non-finite values.
Results may differ from a plain program's by a relative error of at most 0.0036.
Values may be sent and summed in bfloat16 or wider, within the bound.
No kernel may reach another device: no remote copies, remote signals or barrier semaphores. Data moves between devices by JAX's collectives and lax.ppermute only.
A program may use at most 64 MiB of HBM per device.

v0:
```python
import jax
import jax.numpy as jnp
from jax import lax
from jax.sharding import PartitionSpec as P

SIDE = 128
KEEP = 1024


def hadamard(order, dtype):
    indices = jnp.arange(order, dtype=jnp.int32)
    common = indices[:, None] & indices[None, :]
    parity = jnp.zeros((order, order), jnp.int32)
    for position in range(order.bit_length() - 1):
        parity = parity ^ common >> position & 1
    return (1 - 2 * parity).astype(dtype)


def against(left, right):
    return jnp.dot(left, right.T, preferred_element_type=jnp.float32)


def two_factor(spread):
    height = spread.shape[0]
    flat = spread.reshape(height * SIDE, SIDE)
    inner = jnp.dot(flat, hadamard(SIDE, jnp.bfloat16), preferred_element_type=jnp.float32).reshape(
        height, SIDE, SIDE
    )
    outer = jnp.einsum(
        "rak,aj->rjk", inner, hadamard(SIDE, jnp.float32), precision=lax.Precision.HIGHEST
    )
    return outer.reshape(height, SIDE * SIDE)


def per_device(theta, signs, kept):
    scaled = theta * signs.astype(jnp.bfloat16)[None, :]
    spread = lax.all_to_all(scaled, "col", split_axis=0, concat_axis=1, tiled=True)
    transformed = two_factor(spread) / SIDE
    sketch = jnp.take(transformed, kept, axis=1).astype(jnp.bfloat16)
    own_rows = sketch.shape[0]
    half_rows = lax.all_gather(sketch, "col", axis=0, tiled=True)
    gram = against(sketch, lax.all_gather(half_rows, "row", axis=0, tiled=True))
    return (gram / KEEP).reshape(1, 1, own_rows, gram.shape[1])


def solution(mesh):
    return jax.shard_map(
        per_device,
        mesh=mesh,
        in_specs=(P(("real", "row"), "col"), P(("real", "col")), P()),
        out_specs=P(("real", "row"), "col", None, None),
        check_vma=False,
    )
```

profile of v0, /device:TPU:0, one launch (start us, length us, event | category | flops | bytes accessed | tf_op | source)
XLA Modules:
  0.0 69.4 jit_solution(3105334876577274971)
XLA Ops:
  0.0 0.7 %convert_element_type.13 = bf16[2048]{0:T(1024)(128)(2,1)S(1)} convert(s32[2048]{0:T(1024)} %param.4) | non-fusion elementwise | flops 2048 | bytes 12288 | tf_op jit(solution)/shard_map/convert_element_type | solution.py:36
  0.7 1.9 %broadcast_multiply_fusion = bf16[128,2048]{1,0:T(8,128)(2,1)} fusion(bf16[128,2048]{1,0:T(8,128)(2,1)} %param.3, bf16[2048]{0:T(1024)(128)(2,1)S(1)} %convert_element_type.13), kind=kLoop, calls=%fused_computation.6 | loop fusion | flops 262144 | bytes 1052672 | tf_op jit(solution)/shard_map/mul | solution.py:36
  2.6 7.3 %all-to-all-start = ((bf16[8,16,2048]{2,1,0:T(8,128)(2,1)}), bf16[8,16,2048]{2,1,0:T(8,128)(2,1)S(1)}, u32[]{:S(2)}, u32[]{:S(2)}) async-start(bf16[8,16,2048]{2,1,0:T(8,128)(2,1)} %bitcast.1), calls=%async_computation | async-start | bytes 1048576 | tf_op jit(solution)/shard_map/all_to_all | solution.py:37
  9.8 0.7 compare_and_fusion
  10.5 0.7 fusion.7
  11.2 13.1 %all-to-all-done = bf16[8,16,2048]{2,1,0:T(8,128)(2,1)S(1)} async-done(((bf16[8,16,2048]{2,1,0:T(8,128)(2,1)}), bf16[8,16,2048]{2,1,0:T(8,128)(2,1)S(1)}, u32[]{:S(2)}, u32[]{:S(2)}) %all-to-all-start) | async-done | bytes 524320 | tf_op jit(solution)/shard_map/all_to_all | solution.py:37
  24.3 0.3 copy.7
  24.6 0.2 dot_general.11
  24.9 0.3 fusion.4
  25.2 1.1 %fusion = bf16[16,128,128]{2,1,0:T(8,128)(2,1)S(1)} fusion(f32[16,128,128]{2,1,0:T(8,128)S(1)} %fusion.4), kind=kOutput, calls=%fused_computation.2 | convolution fusion | flops 403570688 | bytes 1572864 | tf_op jit(solution)/shard_map/rak,aj->rjk/dot_general | solution.py:29
  26.3 3.2 %copy.13 = bf16[16,128,128]{0,2,1:T(8,128)(2,1)} copy(bf16[16,128,128]{2,1,0:T(8,128)(2,1)S(1)} %fusion) | data formatting | bytes 1048576 | tf_op jit(solution)/shard_map/div | solution.py:38
  29.5 5.6 %gather_fusion = bf16[1024,16]{1,0:T(8,128)(2,1)S(1)} fusion(bf16[16,16384]{0,1:T(8,128)(2,1)} %bitcast.18, s32[1024]{0:T(1024)S(1)} %fusion.7), kind=kCustom, calls=%fused_computation | custom fusion | bytes 69632 | tf_op jit(solution)/shard_map/jit(_take)/gather | solution.py:39
  35.1 0.2 fusion.22
  35.3 0.1 copy.10
  35.4 30.7 %all_gather.6 = bf16[128,1024]{1,0:T(8,128)(2,1)S(1)} all-gather(bf16[16,1024]{1,0:T(8,128)(2,1)S(1)} %copy.10), channel_id=1, replica_groups=mesh['real'=2,'col'=8,'row'=2] {'col'}, dimensions={0}, use_global_device_ids=true | all-gather | bytes 294912 | tf_op jit(solution)/shard_map/all_gather | solution.py:41
  66.1 2.2 %all_gather.7 = bf16[256,1024]{1,0:T(8,128)(2,1)S(1)} all-gather(bf16[128,1024]{1,0:T(8,128)(2,1)S(1)} %all_gather.6), channel_id=1, replica_groups=mesh['real'=2,'col'=8,'row'=2] {'row'}, dimensions={0}, use_global_device_ids=true | all-gather | bytes 786432 | tf_op jit(solution)/shard_map/all_gather | solution.py:42
  68.3 1.1 %fusion.1 = f32[1,1,16,256]{3,2,1,0:T(8,128)} fusion(bf16[256,1024]{1,0:T(8,128)(2,1)S(1)} %all_gather.7, bf16[1024,16]{1,0:T(8,128)(2,1)S(1)} %gather_fusion, pred[1024]{0:T(1024)(128)(4,1)S(1)} %compare_and_fusion), kind=kOutput, calls=%fused_computation.4 | convolution fusion | flops 8409088 | bytes 574464 | tf_op jit(solution)/shard_map/dot_general | solution.py:20
Async XLA Ops:
  2.6 21.8 %all-to-all-start = ((bf16[8,16,2048]{2,1,0:T(8,128)(2,1)}), bf16[8,16,2048]{2,1,0:T(8,128)(2,1)S(1)}, u32[]{:S(2)}, u32[]{:S(2)}) async-start(bf16[8,16,2048]{2,1,0:T(8,128)(2,1)} %bitcast.1), calls=%async_computation | async-start | bytes 1048576 | tf_op jit(solution)/shard_map/all_to_all | solution.py:37
where the time goes:
time: 69.8 us; the launch traced here: 69.4 us
  blocking collectives  32.9 us (47%)
  waiting for transfers between devices  13.1 us (19%)
  local copies, waits for them, and re-layouts  9.42 us (13%)
  starting transfers between devices  7.28 us (10%)
  other arithmetic  4.14 us (6%)
  matrix products  2.5 us (4%)
    all_gather x1, blocking collectives, per_device(): half_rows = lax.all_gather(sketch, 'col', axis=0, tiled=True)  30.7 us
    all_to_all x1, waiting for transfers between devices, per_device(): lax.all_to_all(scaled, 'col', split_axis=0, concat_axis=1, tiled=True)  13.1 us
    all_to_all x1, starting transfers between devices, per_device(): lax.all_to_all(scaled, 'col', split_axis=0, concat_axis=1, tiled=True)  7.28 us
    gather x1, local copies, waits for them, and re-layouts, per_device(): sketch = jnp.take(transformed, kept, axis=1).astype(jnp.bfloat16)  5.6 us
    div x1, local copies, waits for them, and re-layouts, per_device(): transformed = two_factor(spread) / SIDE  3.17 us
    all_gather x1, blocking collectives, per_device(): gram = against(sketch, lax.all_gather(half_rows, 'row', axis=0, tiled=True))  2.17 us
    mul x1, other arithmetic, per_device(): scaled = theta * signs.astype(jnp.bfloat16)[None, :]  1.86 us
  transfers between devices with their start and end apart: 1, of which 1 were waited for; matrix products, arithmetic and copies ran while one was open for 2% of the time, Pallas kernels for 0%

commit v1 on v0

--- a/solution.py
+++ b/solution.py
@@ -34,7 +34,9 @@
 
 def per_device(theta, signs, kept):
     scaled = theta * signs.astype(jnp.bfloat16)[None, :]
-    spread = lax.all_to_all(scaled, "col", split_axis=0, concat_axis=1, tiled=True)
+    parts = jnp.split(scaled, lax.axis_size("col"), axis=0)
+    received = lax.all_to_all(jnp.stack(parts), "col", 0, 0)
+    spread = jnp.concatenate(received, axis=1)
     transformed = two_factor(spread) / SIDE
     sketch = jnp.take(transformed, kept, axis=1).astype(jnp.bfloat16)
     own_rows = sketch.shape[0]

time: 69.8 us -> 74 us (1.060)
  local copies, waits for them, and re-layouts: 9.42 us -> 14.4 us
  other arithmetic: 4.14 us -> 3.37 us
    unnamed x0 -> x7, local copies, waits for them, and re-layouts: none -> 4.37 us
    mul x1, other arithmetic: 1.86 us -> 1.08 us  [per_device(): scaled = theta * signs.astype(jnp.bfloat16)[None, :]]
where the time goes in v1:
time: 74 us; the launch traced here: 73.6 us
  blocking collectives  32.9 us (44%)
  local copies, waits for them, and re-layouts  14.4 us (19%)
  waiting for transfers between devices  13.1 us (18%)
  starting transfers between devices  7.28 us (10%)
  other arithmetic  3.37 us (5%)
  matrix products  2.52 us (3%)
    all_gather x1, blocking collectives, per_device(): half_rows = lax.all_gather(sketch, 'col', axis=0, tiled=True)  30.7 us
    all_to_all x1, waiting for transfers between devices, per_device(): received = lax.all_to_all(jnp.stack(parts), 'col', 0, 0)  13.1 us
    all_to_all x1, starting transfers between devices, per_device(): received = lax.all_to_all(jnp.stack(parts), 'col', 0, 0)  7.28 us
    gather x1, local copies, waits for them, and re-layouts, per_device(): sketch = jnp.take(transformed, kept, axis=1).astype(jnp.bfloat16)  5.6 us
    unnamed x7, local copies, waits for them, and re-layouts  4.37 us
    div x1, local copies, waits for them, and re-layouts, per_device(): transformed = two_factor(spread) / SIDE  3.17 us
    all_gather x1, blocking collectives, per_device(): gram = against(sketch, lax.all_gather(half_rows, 'row', axis=0, tiled=True))  2.17 us
  transfers between devices with their start and end apart: 1, of which 1 were waited for; matrix products, arithmetic and copies ran while one was open for 2% of the time, Pallas kernels for 0%

profile of v1, /device:TPU:0, one launch (start us, length us, event | category | flops | bytes accessed | tf_op | source)
XLA Modules:
  0.0 73.6 jit_solution(7993746374334305770)
XLA Ops:
  0.0 0.7 convert_element_type.13
  0.7 1.1 %broadcast_multiply_fusion = bf16[128,2048]{1,0:T(8,128)(2,1)S(1)} fusion(bf16[128,2048]{1,0:T(8,128)(2,1)} %param.3, bf16[2048]{0:T(1024)(128)(2,1)S(1)} %convert_element_type.13), kind=kLoop, calls=%fused_computation.6 | loop fusion | flops 262144 | bytes 1052672 | tf_op jit(solution)/shard_map/mul | solution.py:36
  1.8 0.6 fusion.9
  2.4 0.6 fusion.8
  3.0 0.6 fusion.7
  3.6 0.6 fusion.6
  4.3 0.6 fusion.5
  4.9 0.6 fusion.4
  5.5 0.6 fusion.3
  6.2 0.6 fusion.2
  6.8 7.3 %all-to-all-start = ((bf16[8,16,2048]{2,1,0:T(8,128)(2,1)}), bf16[8,16,2048]{2,1,0:T(8,128)(2,1)S(1)}, u32[]{:S(2)}, u32[]{:S(2)}) async-start(bf16[8,16,2048]{2,1,0:T(8,128)(2,1)} %fusion.2), calls=%async_computation | async-start | bytes 1048576 | tf_op jit(solution)/shard_map/all_to_all | solution.py:38
  14.1 0.7 compare_and_fusion
  14.7 0.7 fusion.15
  15.4 13.1 %all-to-all-done = bf16[8,16,2048]{2,1,0:T(8,128)(2,1)S(1)} async-done(((bf16[8,16,2048]{2,1,0:T(8,128)(2,1)}), bf16[8,16,2048]{2,1,0:T(8,128)(2,1)S(1)}, u32[]{:S(2)}, u32[]{:S(2)}) %all-to-all-start) | async-done | bytes 524320 | tf_op jit(solution)/shard_map/all_to_all | solution.py:38
  28.5 0.3 copy.7
  28.8 0.2 dot_general.11
  29.1 0.3 fusion.12
  29.4 1.1 %fusion = bf16[16,128,128]{2,1,0:T(8,128)(2,1)S(1)} fusion(f32[16,128,128]{2,1,0:T(8,128)S(1)} %fusion.12), kind=kOutput, calls=%fused_computation.2 | convolution fusion | flops 403570688 | bytes 1572864 | tf_op jit(solution)/shard_map/rak,aj->rjk/dot_general | solution.py:29
  30.5 3.2 %copy.13 = bf16[16,128,128]{0,2,1:T(8,128)(2,1)} copy(bf16[16,128,128]{2,1,0:T(8,128)(2,1)S(1)} %fusion) | data formatting | bytes 1048576 | tf_op jit(solution)/shard_map/div | solution.py:40
  33.7 5.6 %gather_fusion = bf16[1024,16]{1,0:T(8,128)(2,1)S(1)} fusion(bf16[16,16384]{0,1:T(8,128)(2,1)} %bitcast.49, s32[1024]{0:T(1024)S(1)} %fusion.15), kind=kCustom, calls=%fused_computation | custom fusion | bytes 69632 | tf_op jit(solution)/shard_map/jit(_take)/gather | solution.py:41
  39.3 0.2 fusion.30
  39.5 0.1 copy.10
  39.6 30.7 %all_gather.6 = bf16[128,1024]{1,0:T(8,128)(2,1)S(1)} all-gather(bf16[16,1024]{1,0:T(8,128)(2,1)S(1)} %copy.10), channel_id=1, replica_groups=mesh['real'=2,'col'=8,'row'=2] {'col'}, dimensions={0}, use_global_device_ids=true | all-gather | bytes 294912 | tf_op jit(solution)/shard_map/all_gather | solution.py:43
  70.3 2.2 %all_gather.7 = bf16[256,1024]{1,0:T(8,128)(2,1)S(1)} all-gather(bf16[128,1024]{1,0:T(8,128)(2,1)S(1)} %all_gather.6), channel_id=1, replica_groups=mesh['real'=2,'col'=8,'row'=2] {'row'}, dimensions={0}, use_global_device_ids=true | all-gather | bytes 786432 | tf_op jit(solution)/shard_map/all_gather | solution.py:44
  72.5 1.1 %fusion.1 = f32[1,1,16,256]{3,2,1,0:T(8,128)} fusion(bf16[256,1024]{1,0:T(8,128)(2,1)S(1)} %all_gather.7, bf16[1024,16]{1,0:T(8,128)(2,1)S(1)} %gather_fusion, pred[1024]{0:T(1024)(128)(4,1)S(1)} %compare_and_fusion), kind=kOutput, calls=%fused_computation.4 | convolution fusion | flops 8409088 | bytes 574464 | tf_op jit(solution)/shard_map/dot_general | solution.py:20
Async XLA Ops:
  6.8 21.8 %all-to-all-start = ((bf16[8,16,2048]{2,1,0:T(8,128)(2,1)}), bf16[8,16,2048]{2,1,0:T(8,128)(2,1)S(1)}, u32[]{:S(2)}, u32[]{:S(2)}) async-start(bf16[8,16,2048]{2,1,0:T(8,128)(2,1)} %fusion.2), calls=%async_computation | async-start | bytes 1048576 | tf_op jit(solution)/shard_map/all_to_all | solution.py:38
